TPU v7x, 32 devices: a whole 2x2x4 slice. The times are simulated.
32 devices in a mesh: seq: 16 (over z, y, x), tp: 2 (over core).
Axes of the slice: x: 2, y: 2, z: 4, core: 2. Of those that a mesh axis runs over, the one named last changes fastest.
Arguments:
- tokens: bfloat16 [8192, 2048], P('seq', 'tp'), may hold values from -6 to 6
- ln_gain: bfloat16 [2048], replicated, may hold values from 0.5 to 4.1
- w_qkv: bfloat16 [3, 2048, 2048], P(None, None, 'tp'), may hold values from -0.15467961 to 0.15467961
- w_out: bfloat16 [2048, 2048], P('tp'), may hold values from -0.1875 to 0.1875
Outputs:
- mixed: bfloat16 [8192, 2048], P('seq', 'tp')
All inputs are finite; a program needn't handle non-finite values.
Results may differ from a plain program's by a relative error of at most 0.011.
Values may be sent and summed in bfloat16 or wider, within the bound.
A program may use at most 256 MiB of HBM per device.

v0:
```python
import functools
import math

import jax
import jax.numpy as jnp
from jax import lax
from jax.experimental import pallas as pl
from jax.experimental.pallas import tpu as pltpu
from jax.sharding import PartitionSpec as P

HEAD_DIM = 128
CHUNK = 2048
MESH = pl.DeviceIdType.MESH
ANY = pl.BlockSpec(memory_space=pl.ANY)


def remote(src, dst, send, recv, seq, tp):
    return pltpu.make_async_remote_copy(
        src_ref=src, dst_ref=dst, send_sem=send, recv_sem=recv, device_id=(seq, tp), device_id_type=MESH
    )


def put(src, dst, send, recv, seq, tp, own):
    @pl.when(own)
    def _():
        pltpu.make_async_copy(src, dst, recv).start()

    @pl.when(jnp.logical_not(own))
    def _():
        remote(src, dst, send, recv, seq, tp).start()


def project_kernel(
    n, heads, tok, gain, w, q_out, kv_out,
    pair, normed, wbuf, xq, xkv, wsem, psem, qsend, kvsend, qrecv, kvrecv, fsend, frecv,
):
    me, core = lax.axis_index("seq"), lax.axis_index("tp")
    other = 1 - core
    rows, feats = tok.shape
    half = rows // 2
    blocks = heads // 2
    width = 2 * HEAD_DIM

    mine = pltpu.make_async_copy(tok, pair.at[core], psem.at[0])
    mine.start()
    swap = remote(tok, pair.at[core], psem.at[1], psem.at[2], me, other)
    swap.start()

    def wcopy(b, j):
        return pltpu.make_async_copy(w.at[j, :, pl.ds(pl.multiple_of(b * width, width), width)], wbuf.at[b, j], wsem.at[b, j])

    def fetch(i, carry):
        for j in range(3):
            wcopy(lax.rem(lax.rem(me // 2, blocks) + i, blocks), j).start()
        return carry

    lax.fori_loop(0, blocks, fetch, 0)
    mine.wait()
    swap.wait()

    step = 32

    def norm(i, carry):
        at = pl.ds(pl.multiple_of(i * step, step), step)
        a = pair[0, at, :].astype(jnp.float32)
        b = pair[1, at, :].astype(jnp.float32)
        average = (jnp.sum(a, axis=1, keepdims=True) + jnp.sum(b, axis=1, keepdims=True)) / (2 * feats)
        second = (jnp.sum(a * a, axis=1, keepdims=True) + jnp.sum(b * b, axis=1, keepdims=True)) / (2 * feats)
        scale = lax.rsqrt(second - average * average + 1e-06)
        normed[at, :feats] = ((a - average) * scale * gain[0:1, :feats]).astype(jnp.bfloat16)
        normed[at, feats:] = ((b - average) * scale * gain[0:1, feats:]).astype(jnp.bfloat16)
        return carry

    lax.fori_loop(0, rows // step, norm, 0)

    def sends(h, wait):
        chip = core * heads + h
        for u in range(2):
            own = jnp.logical_and(chip == me, core == u)
            at = pl.ds(u * half, half)
            args_q = (xq.at[h, at], q_out.at[me], qsend.at[h, u], qrecv.at[me], chip, u)
            args_kv = (xkv.at[h, at], kv_out.at[u, me], kvsend.at[h, u], kvrecv.at[me], chip, u)
            if wait:

                @pl.when(jnp.logical_not(own))
                def _():
                    remote(*args_q).wait_send()
                    remote(*args_kv).wait_send()
            else:
                put(*args_kv, own)
                put(*args_q, own)

    factor = HEAD_DIM ** (-0.5) * math.log2(math.e)

    first = lax.rem(me // 2, blocks)

    def block_at(i):
        return lax.rem(first + i, blocks)

    def send_block(b):
        near = lax.rem(me, 2)
        sends(2 * b + near, False)
        sends(2 * b + 1 - near, False)

    def project(i, carry):
        b = block_at(i)
        for j in range(3):
            wcopy(b, j).wait()
            got = jnp.dot(normed[...], wbuf[b, j], preferred_element_type=jnp.float32)
            if j == 0:
                got = got * factor
            got = got.astype(jnp.bfloat16)
            for side in range(2):
                part = got[:, side * HEAD_DIM : (side + 1) * HEAD_DIM]
                if j == 0:
                    xq[2 * b + side] = part
                else:
                    xkv[2 * b + side, :, (j - 1) * HEAD_DIM : j * HEAD_DIM] = part

        @pl.when(i > 0)
        def _():
            send_block(block_at(i - 1))

        return carry

    lax.fori_loop(0, blocks, project, 0)
    send_block(block_at(blocks - 1))

    def got_kv(s):
        return remote(xkv.at[0, pl.ds(0, half)], kv_out.at[core, s], kvsend.at[0, 0], kvrecv.at[s], me, other)

    def forward(s):
        return remote(kv_out.at[core, s], kv_out.at[core, s], fsend.at[s], frecv.at[s], me, other)

    def pass_on(i, carry):
        s = lax.rem(me + i, n)
        got_kv(s).wait_recv()
        forward(s).start()
        return carry

    lax.fori_loop(0, n, pass_on, 0)

    def finish(s, carry):
        remote(xq.at[0, pl.ds(0, half)], q_out.at[s], qsend.at[0, 0], qrecv.at[s], me, other).wait_recv()
        forward(s).wait_send()
        remote(kv_out.at[other, s], kv_out.at[other, s], fsend.at[s], frecv.at[s], me, other).wait_recv()
        return carry

    lax.fori_loop(0, n, finish, 0)

    def drain(h, carry):
        sends(h, True)
        return carry

    lax.fori_loop(0, heads, drain, 0)


def project(tokens, gain, w_qkv, n):
    rows, feats = tokens.shape
    heads = w_qkv.shape[2] // HEAD_DIM
    half = rows // 2
    bf = jnp.bfloat16
    dma = pltpu.SemaphoreType.DMA
    return pl.pallas_call(
        functools.partial(project_kernel, n, heads),
        out_shape=(
            jax.ShapeDtypeStruct((n, half, HEAD_DIM), bf),
            jax.ShapeDtypeStruct((2, n, half, 2 * HEAD_DIM), bf),
        ),
        in_specs=[ANY, pl.BlockSpec(memory_space=pltpu.VMEM), ANY],
        out_specs=(ANY, ANY),
        scratch_shapes=[
            pltpu.VMEM((2, rows, feats), bf),
            pltpu.VMEM((rows, 2 * feats), bf),
            pltpu.VMEM((heads // 2, 3, 2 * feats, 2 * HEAD_DIM), bf),
            pltpu.VMEM((heads, rows, HEAD_DIM), bf),
            pltpu.VMEM((heads, rows, 2 * HEAD_DIM), bf),
            dma((heads // 2, 3)), dma((3,)), dma((heads, 2)), dma((heads, 2)),
            dma((n,)), dma((n,)), dma((n,)), dma((n,)),
        ],
        compiler_params=pltpu.CompilerParams(has_side_effects=True, vmem_limit_bytes=48 * 1024 * 1024),
        name="project",
    )(tokens, gain, w_qkv)


def attend_rows(chunk, group, queries, kv_ref, vones):
    keys = kv_ref.shape[0]

    def body(i, carry):
        at = pl.ds(pl.multiple_of(i * chunk, chunk), chunk)
        kept = []
        scores = [
            lax.dot_general(q, kv_ref[at, :HEAD_DIM], (((1,), (1,)), ((), ())), preferred_element_type=jnp.float32)
            for q in queries
        ]
        for (top, total), s in zip(carry, scores):
            high = jnp.maximum(top, jnp.max(s, axis=1, keepdims=True))
            p = jnp.exp2((s - high).astype(jnp.bfloat16))
            add = jnp.dot(p, vones[at, :], preferred_element_type=jnp.float32)
            kept.append((high, total * jnp.exp2(top - high) + add))
        return tuple(kept)

    start = tuple(
        (jnp.full((group, 1), -1e30, jnp.float32), jnp.zeros((group, 2 * HEAD_DIM), jnp.float32)) for _ in queries
    )
    done = lax.fori_loop(0, keys // chunk, body, start, unroll=2)
    return [(total[:, :HEAD_DIM] / total[:, HEAD_DIM:]).astype(jnp.bfloat16) for _, total in done]


def output_kernel(n, heads, queries, kv, tok, w, out, vones, ctx, held, sent, came, send, recv, psem):
    me, core = lax.axis_index("seq"), lax.axis_index("tp")
    other = 1 - core
    rows, feats = tok.shape
    half = rows // 2
    home, slot = me // heads, lax.rem(me, heads)

    def place(u, h):
        return held.at[
            pl.ds(pl.multiple_of(u * half, half), half), pl.ds(pl.multiple_of(h * HEAD_DIM, HEAD_DIM), HEAD_DIM)
        ]

    def give(i, wait):
        s = lax.rem(me + i, n)
        own = jnp.logical_and(s == me, home == core)
        args = (ctx.at[s], place(core, slot), send.at[s], recv.at[core, slot], s, home)
        if wait:

            @pl.when(jnp.logical_not(own))
            def _():
                remote(*args).wait_send()
        else:
            put(*args, own)

    vones[:, :HEAD_DIM] = kv[:, HEAD_DIM:]
    vones[:, HEAD_DIM:] = jnp.ones((kv.shape[0], HEAD_DIM), jnp.bfloat16)
    chunk = math.gcd(CHUNK, kv.shape[0])

    def attend(i, carry):
        turns = [2 * i + 1, 2 * i + 2]
        sources = [lax.rem(me + turn, n) for turn in turns]
        got = attend_rows(chunk, half, [queries[s] for s in sources], kv, vones)
        for s, rows_done in zip(sources, got):
            ctx[s] = rows_done

        @pl.when(i > 0)
        def _():
            give(2 * i - 1, False)
            give(2 * i, False)

        return carry

    lax.fori_loop(0, n // 2, attend, 0)
    give(n - 1, False)
    give(n, False)

    def arrive(i, carry):
        u, h = i // heads, lax.rem(i, heads)
        remote(ctx.at[0], place(u, h), send.at[0], recv.at[u, h], me, other).wait_recv()
        return carry

    lax.fori_loop(0, 2 * heads, arrive, 0)

    width = 2 * HEAD_DIM

    def product(side, i):
        at = pl.ds(pl.multiple_of(side * feats + i * width, width), width)
        return jnp.dot(held[...], w[:, at], preferred_element_type=jnp.float32)

    pieces = feats // width

    def share(i):
        return remote(sent.at[i], came.at[i], psem.at[0, i], psem.at[1, i], me, other)

    def theirs(i, carry):
        sent[i] = product(other, i).astype(jnp.bfloat16)

        @pl.when(i > 0)
        def _():
            share(i - 1).start()

        return carry

    lax.fori_loop(0, pieces, theirs, 0)
    share(pieces - 1).start()

    def ours(i, carry):
        at = pl.ds(pl.multiple_of(i * width, width), width)
        got = product(core, i)
        share(i).wait_recv()
        out[:, at] = (tok[:, at].astype(jnp.float32) + (got + came[i].astype(jnp.float32))).astype(jnp.bfloat16)
        return carry

    lax.fori_loop(0, pieces, ours, 0)

    def drain(i, carry):
        give(i + 1, True)
        return carry

    lax.fori_loop(0, n, drain, 0)
    for i in range(pieces):
        share(i).wait_send()


def output(q, kv, tokens, w_out, n):
    rows, feats = tokens.shape
    heads = w_out.shape[0] // HEAD_DIM
    bf = jnp.bfloat16
    dma = pltpu.SemaphoreType.DMA
    vm = pl.BlockSpec(memory_space=pltpu.VMEM)
    pieces = feats // (2 * HEAD_DIM)
    return pl.pallas_call(
        functools.partial(output_kernel, n, heads),
        out_shape=jax.ShapeDtypeStruct((rows, feats), bf),
        in_specs=[vm, vm, vm, vm],
        out_specs=vm,
        scratch_shapes=[
            pltpu.VMEM(kv.shape, bf),
            pltpu.VMEM(q.shape, bf),
            pltpu.VMEM((rows, heads * HEAD_DIM), bf),
            pltpu.VMEM((pieces, rows, 2 * HEAD_DIM), bf),
            pltpu.VMEM((pieces, rows, 2 * HEAD_DIM), bf),
            dma((n,)), dma((2, heads)), dma((2, pieces)),
        ],
        compiler_params=pltpu.CompilerParams(has_side_effects=True, vmem_limit_bytes=56 * 1024 * 1024),
        name="output",
    )(q, kv, tokens, w_out)


def head_per_chip(n, tokens, ln_gain, w_qkv, w_out):
    gain = ln_gain.astype(jnp.float32).reshape(1, -1)
    q, kv = project(tokens, gain, w_qkv, n)
    half = q.shape[1]
    return output(q, kv.reshape(2 * n * half, 2 * HEAD_DIM), tokens, w_out, n)


def attend_block(totals, queries, block_kv, factor):
    running, denoms, accum = totals
    heads_here = queries.shape[1]
    keys_part = block_kv[0].reshape(block_kv.shape[1], heads_here, queries.shape[2])
    vals_part = block_kv[1].reshape(block_kv.shape[1], heads_here, queries.shape[2])
    scores = (
        jnp.einsum("thc,shc->ths", queries, keys_part, preferred_element_type=jnp.float32) * factor
    )
    highest = jnp.maximum(running, jnp.max(scores, axis=2))
    expon = jnp.exp(scores - highest[:, :, None])
    denoms = jnp.sum(expon, axis=2)
    weights = expon.astype(jnp.bfloat16)
    accum = jnp.einsum("ths,shc->thc", weights, vals_part, preferred_element_type=jnp.float32)
    return (highest, denoms, accum)


def start_totals(rows, heads_count):
    return (
        jnp.full((rows, heads_count), -1e30, jnp.float32),
        jnp.zeros((rows, heads_count), jnp.float32),
        jnp.zeros((rows, heads_count, HEAD_DIM), jnp.float32),
    )


def on_device(tokens, ln_gain, w_qkv, w_out):
    tok_rows = tokens.shape[0]
    whole = lax.all_gather(tokens, "tp", axis=1, tiled=True)
    values = whole.astype(jnp.float32)
    average = jnp.mean(values, axis=1, keepdims=True)
    second = jnp.mean(values * values, axis=1, keepdims=True)
    normed = (
        (values - average)
        * lax.rsqrt(second - average * average + 1e-06)
        * ln_gain.astype(jnp.float32)
    ).astype(jnp.bfloat16)
    projected = jnp.einsum("td,jdc->jtc", normed, w_qkv, preferred_element_type=jnp.float32).astype(
        jnp.bfloat16
    )
    heads_here = w_qkv.shape[2] // HEAD_DIM
    factor = HEAD_DIM ** (-0.5)
    queries = projected[0].reshape(tok_rows, heads_here, HEAD_DIM)
    keys_vals = projected[1:3]
    initial = start_totals(tok_rows, heads_here)
    final = attend_block(
        initial, queries, lax.all_gather(keys_vals, "seq", axis=1, tiled=True), factor
    )
    context = (
        (final[2] / final[1][:, :, None])
        .reshape(tok_rows, heads_here * HEAD_DIM)
        .astype(jnp.bfloat16)
    )
    summed = lax.psum_scatter(
        lax.dot_general(
            w_out, context, (((0,), (1,)), ((), ())), preferred_element_type=jnp.float32
        ).astype(jnp.bfloat16),
        "tp",
        scatter_dimension=0,
        tiled=True,
    ).astype(jnp.float32)
    return (tokens.astype(jnp.float32) + summed.T).astype(jnp.bfloat16)


def solution(mesh):
    in_specs = (P("seq", "tp"), P(), P(None, None, "tp"), P("tp", None))
    out_specs = P("seq", "tp")
    n, cores = mesh.shape["seq"], mesh.shape["tp"]

    def run(tokens, ln_gain, w_qkv, w_out):
        heads = w_qkv.shape[2] // HEAD_DIM
        if cores == 2 and heads * cores == n and heads % 2 == 0:
            return head_per_chip(n, tokens, ln_gain, w_qkv, w_out)
        return on_device(tokens, ln_gain, w_qkv, w_out)

    return jax.shard_map(run, mesh=mesh, in_specs=in_specs, out_specs=out_specs, check_vma=False)
```

profile of v0, /device:TPU:29, one launch (start us, length us, event | category | flops | bytes accessed | tf_op | source)
XLA Modules:
  0.0 164.2 jit_solution(1413800122220608608)
XLA Ops:
  0.0 0.7 reshape.11
  0.7 0.0 copy-start
  0.7 1.2 copy-done
  1.9 79.4 %project.1 = (bf16[16,256,128]{2,1,0:T(8,128)(2,1)S(1)}, bf16[2,16,256,256]{3,2,1,0:T(8,128)(2,1)}) custom-call(bf16[512,1024]{1,0:T(8,128)(2,1)S(1)} %copy-done, f32[1,2048]{1,0:T(1,128)S(1)} %bitcast.2, bf16[3,2048,1024]{2,1,0:T(8,128)(2,1)} %w.2), custom_call_target="tpu_custom_call" | custom-call | tf_op jit(solution)/shard_map/project/pallas_call | solution.py:164
  81.3 0.0 copy-start.1
  81.3 1.0 copy-done.1
  82.3 79.6 %output.1 = bf16[512,1024]{1,0:T(8,128)(2,1)} custom-call(bf16[16,256,128]{2,1,0:T(8,128)(2,1)} %copy-done.1, bf16[8192,256]{1,0:T(8,128)(2,1)} %bitcast.3, bf16[512,1024]{1,0:T(8,128)(2,1)} %tok.3, bf16[1024,2048]{1,0:T(8,128)(2,1)} %w.3), custom_call_target="tpu_custom_call" | custom-call | tf_op jit(solution)/shard_map/output/pallas_call | solution.py:311
  161.9 2.3 %copy.6 = bf16[512,1024]{1,0:T(8,128)(2,1)} copy(bf16[512,1024]{1,0:T(8,128)(2,1)} %output.1) | data formatting | bytes 2097152
Async XLA Ops:
  0.7 1.2 copy-start
  81.3 1.0 copy-start.1
where the time goes:
time: 166 us; the launch traced here: 164 us
  Pallas kernels  159 us (96%)
  local copies, waits for them, and re-layouts  4.45 us (3%)
    pallas_call x1, Pallas kernels, output(): pl.pallas_call(functools.partial(output_kernel, n, heads), out_shape=jax....  79.6 us
    pallas_call x1, Pallas kernels, project(): pl.pallas_call(functools.partial(project_kernel, n, heads), out_shape=(ja...  79.4 us
    unnamed x5, local copies, waits for them, and re-layouts  4.45 us

commit v1 on v0

v1 whole, which is shorter than its diff:
```python
import functools
import math

import jax
import jax.numpy as jnp
from jax import lax
from jax.experimental import pallas as pl
from jax.experimental.pallas import tpu as pltpu
from jax.sharding import PartitionSpec as P

HEAD_DIM = 128
MESH = pl.DeviceIdType.MESH
ANY = pl.BlockSpec(memory_space=pl.ANY)


def remote(src, dst, send, recv, seq, tp):
    return pltpu.make_async_remote_copy(
        src_ref=src, dst_ref=dst, send_sem=send, recv_sem=recv, device_id=(seq, tp), device_id_type=MESH
    )


def put(src, dst, send, recv, seq, tp, own):
    @pl.when(own)
    def _():
        pltpu.make_async_copy(src, dst, recv).start()

    @pl.when(jnp.logical_not(own))
    def _():
        remote(src, dst, send, recv, seq, tp).start()


def half_kernel(
    n, heads, tok, gain, w_qkv, w_out, out,
    pair, far, normed, wbuf, wout, xq, xk, xv, yq, yk, yv, q_all, k_all, v_all, acc, top, s0, s1, ctx, held, sent, came, kept, res,
    lsem, swap, wsem, xsem, osem, qsend, qrecv, fsend, frecv, csend, crecv, psem,
):
    me, core = lax.axis_index("seq"), lax.axis_index("tp")
    other = 1 - core
    rows, feats = pair.shape[1], pair.shape[2]
    plane = n // 4
    near = n // 2
    piece = rows // plane
    layer, spot = me // plane, lax.rem(me, plane)
    side, inner = me // near, lax.rem(me // plane, 2)
    mate = (3 - layer) * plane + spot
    lane = lax.rem(me, 2)
    index = lax.rem(me, near) // 2
    head = side * plane + spot
    bf, f32 = jnp.bfloat16, jnp.float32

    mine = pltpu.make_async_copy(tok, pair.at[core], lsem.at[0])
    mine.start()
    trade = remote(tok, pair.at[core], swap.at[0], swap.at[1], me, other)
    trade.start()
    wide = 2 * HEAD_DIM
    groups = plane // 2

    def wcopy(b, j):
        at = pl.ds(pl.multiple_of(side * plane * HEAD_DIM + b * wide, wide), wide)
        return pltpu.make_async_copy(w_qkv.at[j, :, at], wbuf.at[b, j], wsem.at[b, j])

    for b in range(groups):
        for j in range(3):
            wcopy(b, j).start()
    fetch_out = pltpu.make_async_copy(w_out, wout, lsem.at[1])
    fetch_out.start()

    acc[...] = jnp.zeros_like(acc)
    top[...] = jnp.full_like(top, -1e30)
    v_all[:, HEAD_DIM:, :] = jnp.ones((v_all.shape[0], v_all.shape[1] - HEAD_DIM, v_all.shape[2]), bf)

    mine.wait()
    trade.wait()

    def part(ref, half, w):
        return ref.at[half, pl.ds(w * piece, piece)]

    def across(w, half):
        return remote(part(pair, half, w), part(far, half, w), xsem.at[0, w, half], xsem.at[1, w, half], mate, core)

    def inside(w, half):
        return remote(part(far, half, w), part(far, half, w), xsem.at[2, w, half], xsem.at[3, w, half], me, other)

    @pl.when(core == inner)
    def _():
        for w in range(plane):
            for half in range(2):
                across(w, half).start()

    step = 32

    def normalize(src, offset, count):
        def norm(i, carry):
            at = pl.ds(pl.multiple_of(offset + i * step, step), step)
            to = pl.ds(pl.multiple_of(i * step, step), step)
            a = src[0, at, :].astype(f32)
            b = src[1, at, :].astype(f32)
            average = (jnp.sum(a, axis=1, keepdims=True) + jnp.sum(b, axis=1, keepdims=True)) / (2 * feats)
            second = (jnp.sum(a * a, axis=1, keepdims=True) + jnp.sum(b * b, axis=1, keepdims=True)) / (2 * feats)
            scale = lax.rsqrt(second - average * average + 1e-06)
            normed[to, :feats] = ((a - average) * scale * gain[0:1, :feats]).astype(bf)
            normed[to, feats:] = ((b - average) * scale * gain[0:1, feats:]).astype(bf)
            return carry

        lax.fori_loop(0, count // step, norm, 0)

    factor = HEAD_DIM ** (-0.5) * math.log2(math.e)

    def deliver(block, h, pieces):
        chip = side * near + core * plane + h
        own = jnp.logical_and(chip == me, core == lane)
        for j, (src, dst) in enumerate(pieces):
            args = (src, dst, qsend.at[block, h, j], qrecv.at[block, index, j], chip, lane)
            put(*args, own)

    def delivered(block, h, pieces):
        chip = side * near + core * plane + h
        own = jnp.logical_and(chip == me, core == lane)

        @pl.when(jnp.logical_not(own))
        def _():
            for j, (src, dst) in enumerate(pieces):
                remote(src, dst, qsend.at[block, h, j], qrecv.at[block, index, j], chip, lane).wait_send()

    def spots(block, u, i):
        if block == 0:
            k_at = u * plane + i
            return q_all.at[i], k_all.at[k_at], v_all.at[k_at, pl.ds(0, HEAD_DIM)]
        k_at = 2 * plane + 2 * (block - 1) + u
        at = pl.ds(pl.multiple_of(i * piece, piece), piece)
        return q_all.at[plane + block - 1, at], k_all.at[k_at, at], v_all.at[k_at, pl.ds(0, HEAD_DIM), at]

    def staged(block, h):
        if block == 0:
            return xq.at[h], xk.at[h], xv.at[h]
        return yq.at[block - 1, h], yk.at[block - 1, h], yv.at[block - 1, h]

    def pieces_of(block, h):
        return list(zip(staged(block, h), spots(block, lane, index)))

    def project(block, count):
        for turn in range(groups):
            b = lax.rem(spot // 2 + turn, groups)
            for j in range(3):
                if block == 0:
                    wcopy(b, j).wait()
                got = jnp.dot(normed[:count, :], wbuf[b, j], preferred_element_type=f32)
                if j == 0:
                    got = got * factor
                for half in range(2):
                    cut = got[:, half * HEAD_DIM : (half + 1) * HEAD_DIM]
                    store = staged(block, 2 * b + half)[j]
                    store[...] = (cut.T if j == 2 else cut).astype(bf)
            for half in range(2):
                h = 2 * b + lax.rem(spot + half, 2)
                deliver(block, h, pieces_of(block, h))

    def wave(w):
        @pl.when(core != inner)
        def _():
            for half in range(2):
                across(w, half).wait_recv()
                inside(w, half).start()

        @pl.when(core == inner)
        def _():
            for half in range(2):
                inside(w, half).wait_recv()

        normalize(far, w * piece, piece)
        project(w + 1, piece)

    def wait_block(block, i):
        for j, (src, dst) in enumerate(zip(staged(block, 0), spots(block, core, i))):
            remote(src, dst, qsend.at[block, 0, j], qrecv.at[block, i, j], me, other).wait_recv()

    def share(slot, u, way):
        at = u * plane + slot if way == 0 else 2 * plane + 2 * slot + u
        sem = slot if way == 0 else plane + slot
        return (
            remote(k_all.at[at], k_all.at[at], fsend.at[sem, 0], frecv.at[sem, 0], me, other),
            remote(
                v_all.at[at, pl.ds(0, HEAD_DIM)], v_all.at[at, pl.ds(0, HEAD_DIM)], fsend.at[sem, 1], frecv.at[sem, 1], me, other
            ),
        )

    def pass_on(slot, way):
        for copy in share(slot, core, way):
            copy.start()

    def from_other(slot, way):
        for copy in share(slot, other, way):
            copy.wait_recv()

    def segment(rects):
        total = sum(nq * nk for _, nq, _, nk in rects)

        def find(t):
            spot_q = spot_k = None
            before = 0
            for q0, nq, k0, nk in rects:
                a = q0 + (t - before) // nk
                b = k0 + lax.rem(t - before, nk)
                if spot_q is None:
                    spot_q, spot_k = a, b
                else:
                    spot_q = jnp.where(t >= before, a, spot_q)
                    spot_k = jnp.where(t >= before, b, spot_k)
                before += nq * nk
            return spot_q, spot_k

        def score(t, s):
            a, b = find(t)
            s[...] = lax.dot_general(k_all[b], q_all[a], (((1,), (1,)), ((), ())), preferred_element_type=f32)

        def weigh(t, s):
            a, b = find(t)
            now = s[...]
            was = top[a]
            high = jnp.maximum(was, jnp.max(now, axis=0, keepdims=True))
            p = jnp.exp2((now - high).astype(bf))
            add = jnp.dot(v_all[b], p, preferred_element_type=f32)
            acc[a] = acc[a] * jnp.exp2(was - high) + add
            top[a] = high

        score(jnp.int32(0), s0)

        def body(i, carry):
            t = 2 * i
            score(t + 1, s1)
            weigh(t, s0)
            score(jnp.minimum(t + 2, total - 1), s0)
            weigh(t + 1, s1)
            return carry

        lax.fori_loop(0, total // 2, body, 0)
        if total % 2:
            weigh(jnp.int32(total - 1), s0)

    def place(l, at):
        return held.at[at, pl.ds(pl.multiple_of(l * HEAD_DIM, HEAD_DIM), HEAD_DIM)]

    def returns(b):
        if b < plane:
            s = side * near + 2 * b + core
            own = jnp.logical_and(s == me, inner == core)
            return [((ctx.at[b], place(head, pl.ds(0, rows)), csend.at[b, 0], crecv.at[head, 0], s, inner), own)]
        w = b - plane
        found = []
        for i in range(plane):
            s = side * near + 2 * i + core
            owner = (3 - s // plane) * plane + lax.rem(s, plane)
            src = ctx.at[b, pl.ds(i * piece, piece)]
            found.append(((src, place(head, pl.ds(w * piece, piece)), csend.at[b, i], crecv.at[head, w], owner, inner), None))
        return found

    def finish(first, count):
        def one(b, carry):
            t = acc[b]
            ctx[b] = (t[:HEAD_DIM] / t[HEAD_DIM : HEAD_DIM + 1]).T.astype(bf)
            return carry

        lax.fori_loop(first, first + count, one, 0)
        for b in range(first, first + count):
            for args, own in returns(b):
                if own is None:
                    remote(*args).start()
                else:
                    put(*args, own)

    normalize(pair, 0, rows)
    project(0, rows)
    wave(0)
    here, there = 2 * inner, 2 * (1 - inner)
    for k in range(2):
        wait_block(0, here + k)
        pass_on(here + k, 0)
    segment([(here, 2, core * plane + here, 2)])
    for k in range(2):
        wait_block(0, there + k)
        pass_on(there + k, 0)
    segment([(here, 2, core * plane + there, 2), (there, 2, core * plane, plane)])
    wave(1)
    for k in range(plane):
        from_other(k, 0)
    segment([(0, plane, other * plane, plane)])

    def take(w):
        for i in range(plane):
            wait_block(w + 1, i)
        pass_on(w, 1)

    for w in range(plane):
        fresh, old = plane + w, 2 * plane + 2 * w
        take(w)
        if w < plane - 1:
            segment([(0, fresh, old + core, 1), (fresh, 1, 0, old), (fresh, 1, old + core, 1)])
            if w + 2 < plane:
                wave(w + 2)
            from_other(w, 1)
            segment([(0, fresh + 1, old + other, 1)])
        else:
            segment([(0, fresh, old + core, 1)])
            from_other(w, 1)
            segment([(plane, plane - 1, old + other, 1)])
            finish(plane, plane - 1)
            segment([(fresh, 1, 0, old + 2)])
            finish(fresh, 1)
            segment([(0, plane, old + other, 1)])
            finish(0, plane)

    fetch_out.wait()
    for k in range(plane):
        l = side * plane + k
        remote(ctx.at[0], place(l, pl.ds(0, rows)), csend.at[0, 0], crecv.at[l, 0], me, other).wait_recv()

    def product(half, w):
        at = pl.ds(pl.multiple_of(half * feats, feats), feats)
        return jnp.dot(held[w * piece : (w + 1) * piece, :], wout[:, at], preferred_element_type=f32)

    def hand(w):
        return remote(sent.at[w], came.at[w], psem.at[0, w], psem.at[1, w], me, other)

    def leave(w):
        at = pl.ds(w * piece, piece)
        return pltpu.make_async_copy(res.at[at], out.at[at], osem.at[w])

    for w in range(plane):
        for k in range(plane):
            l = (1 - side) * plane + k
            at = pl.ds(w * piece, piece)
            remote(ctx.at[0, at], place(l, at), csend.at[0, 0], crecv.at[l, w], me, other).wait_recv()
        sent[w] = product(other, w).astype(bf)
        hand(w).start()
        kept[w * piece : (w + 1) * piece, :] = product(core, w)

    for w in range(plane):
        hand(w).wait_recv()
        at = slice(w * piece, (w + 1) * piece)
        res[at, :] = (pair[core, at, :].astype(f32) + (kept[at, :] + came[w].astype(f32))).astype(bf)
        leave(w).start()

    for block in range(plane + 1):
        for h in range(plane):
            delivered(block, h, pieces_of(block, h))
    for slot in range(plane):
        for way in range(2):
            for copy in share(slot, core, way):
                copy.wait_send()

    @pl.when(core == inner)
    def _():
        for w in range(plane):
            for half in range(2):
                across(w, half).wait_send()

    @pl.when(core != inner)
    def _():
        for w in range(plane):
            for half in range(2):
                inside(w, half).wait_send()

    for b in range(2 * plane):
        for args, own in returns(b):
            if own is None:
                remote(*args).wait_send()
            else:

                @pl.when(jnp.logical_not(own))
                def _():
                    remote(*args).wait_send()

    for w in range(plane):
        hand(w).wait_send()
        leave(w).wait()


def half_per_layer(n, tokens, ln_gain, w_qkv, w_out):
    rows, feats = tokens.shape
    heads = w_qkv.shape[2] // HEAD_DIM
    plane = n // 4
    piece = rows // plane
    bf, f32 = jnp.bfloat16, jnp.float32
    dma = pltpu.SemaphoreType.DMA
    gain = ln_gain.astype(f32).reshape(1, -1)
    chunks = 4 * plane
    blocks = 2 * plane
    extra = HEAD_DIM + 16
    vmem = pltpu.VMEM
    return pl.pallas_call(
        functools.partial(half_kernel, n, heads),
        out_shape=jax.ShapeDtypeStruct((rows, feats), bf),
        in_specs=[ANY, pl.BlockSpec(memory_space=pltpu.VMEM), ANY, ANY],
        out_specs=ANY,
        scratch_shapes=[
            vmem((2, rows, feats), bf),
            vmem((2, rows, feats), bf),
            vmem((rows, 2 * feats), bf),
            vmem((plane // 2, 3, 2 * feats, 2 * HEAD_DIM), bf),
            vmem(w_out.shape, bf),
            vmem((plane, rows, HEAD_DIM), bf),
            vmem((plane, rows, HEAD_DIM), bf),
            vmem((plane, HEAD_DIM, rows), bf),
            vmem((plane, plane, piece, HEAD_DIM), bf),
            vmem((plane, plane, piece, HEAD_DIM), bf),
            vmem((plane, plane, HEAD_DIM, piece), bf),
            vmem((blocks, rows, HEAD_DIM), bf),
            vmem((chunks, rows, HEAD_DIM), bf),
            vmem((chunks, extra, rows), bf),
            vmem((blocks, extra, rows), f32),
            vmem((blocks, 1, rows), f32),
            vmem((rows, rows), f32),
            vmem((rows, rows), f32),
            vmem((blocks, rows, HEAD_DIM), bf),
            vmem((rows, heads * HEAD_DIM), bf),
            vmem((plane, piece, feats), bf),
            vmem((plane, piece, feats), bf),
            vmem((rows, feats), f32),
            vmem((rows, feats), bf),
            dma((2,)), dma((2,)), dma((plane // 2, 3)), dma((4, plane, 2)), dma((plane,)),
            dma((plane + 1, plane, 3)), dma((plane + 1, plane, 3)), dma((blocks, 2)), dma((blocks, 2)),
            dma((blocks, plane)), dma((heads, plane)), dma((2, plane)),
        ],
        compiler_params=pltpu.CompilerParams(has_side_effects=True, vmem_limit_bytes=60 * 1024 * 1024),
        name="sublayer",
    )(tokens, gain, w_qkv, w_out)


def attend_block(totals, queries, block_kv, factor):
    running, denoms, accum = totals
    heads_here = queries.shape[1]
    keys_part = block_kv[0].reshape(block_kv.shape[1], heads_here, queries.shape[2])
    vals_part = block_kv[1].reshape(block_kv.shape[1], heads_here, queries.shape[2])
    scores = (
        jnp.einsum("thc,shc->ths", queries, keys_part, preferred_element_type=jnp.float32) * factor
    )
    highest = jnp.maximum(running, jnp.max(scores, axis=2))
    expon = jnp.exp(scores - highest[:, :, None])
    denoms = jnp.sum(expon, axis=2)
    weights = expon.astype(jnp.bfloat16)
    accum = jnp.einsum("ths,shc->thc", weights, vals_part, preferred_element_type=jnp.float32)
    return (highest, denoms, accum)


def start_totals(rows, heads_count):
    return (
        jnp.full((rows, heads_count), -1e30, jnp.float32),
        jnp.zeros((rows, heads_count), jnp.float32),
        jnp.zeros((rows, heads_count, HEAD_DIM), jnp.float32),
    )


def on_device(tokens, ln_gain, w_qkv, w_out):
    tok_rows = tokens.shape[0]
    whole = lax.all_gather(tokens, "tp", axis=1, tiled=True)
    values = whole.astype(jnp.float32)
    average = jnp.mean(values, axis=1, keepdims=True)
    second = jnp.mean(values * values, axis=1, keepdims=True)
    normed = (
        (values - average)
        * lax.rsqrt(second - average * average + 1e-06)
        * ln_gain.astype(jnp.float32)
    ).astype(jnp.bfloat16)
    projected = jnp.einsum("td,jdc->jtc", normed, w_qkv, preferred_element_type=jnp.float32).astype(
        jnp.bfloat16
    )
    heads_here = w_qkv.shape[2] // HEAD_DIM
    factor = HEAD_DIM ** (-0.5)
    queries = projected[0].reshape(tok_rows, heads_here, HEAD_DIM)
    keys_vals = projected[1:3]
    initial = start_totals(tok_rows, heads_here)
    final = attend_block(
        initial, queries, lax.all_gather(keys_vals, "seq", axis=1, tiled=True), factor
    )
    context = (
        (final[2] / final[1][:, :, None])
        .reshape(tok_rows, heads_here * HEAD_DIM)
        .astype(jnp.bfloat16)
    )
    summed = lax.psum_scatter(
        lax.dot_general(
            w_out, context, (((0,), (1,)), ((), ())), preferred_element_type=jnp.float32
        ).astype(jnp.bfloat16),
        "tp",
        scatter_dimension=0,
        tiled=True,
    ).astype(jnp.float32)
    return (tokens.astype(jnp.float32) + summed.T).astype(jnp.bfloat16)


def solution(mesh):
    in_specs = (P("seq", "tp"), P(), P(None, None, "tp"), P("tp", None))
    out_specs = P("seq", "tp")
    n, cores = mesh.shape["seq"], mesh.shape["tp"]

    def run(tokens, ln_gain, w_qkv, w_out):
        heads = w_qkv.shape[2] // HEAD_DIM
        if cores == 2 and heads * cores == n and n % 8 == 0 and tokens.shape[0] % n == 0:
            return half_per_layer(n, tokens, ln_gain, w_qkv, w_out)
        return on_device(tokens, ln_gain, w_qkv, w_out)

    return jax.shard_map(run, mesh=mesh, in_specs=in_specs, out_specs=out_specs, check_vma=False)
```

time: 166 us -> 138 us (0.83)
  Pallas kernels: 159 us -> 133 us
  local copies, waits for them, and re-layouts: 4.45 us -> 2.26 us
    pallas_call x2 -> x1, Pallas kernels: 159 us -> 133 us  [half_per_layer(): pl.pallas_call(functools.partial(half_kernel, n, heads), out_shape=jax.Sh...]
    unnamed x5 -> x1, local copies, waits for them, and re-layouts: 4.45 us -> 2.26 us
where the time goes in v1:
time: 138 us; the launch traced here: 136 us
  Pallas kernels  133 us (96%)
  local copies, waits for them, and re-layouts  2.26 us (2%)
    pallas_call x1, Pallas kernels, half_per_layer(): pl.pallas_call(functools.partial(half_kernel, n, heads), out_shape=jax.Sh...  133 us

profile of v1, /device:TPU:29, one launch (start us, length us, event | category | flops | bytes accessed | tf_op | source)
XLA Modules:
  0.0 136.2 jit_solution(8949292204825813068)
XLA Ops:
  0.0 1.3 reshape.7
  1.3 132.6 %sublayer.1 = bf16[512,1024]{1,0:T(8,128)(2,1)} custom-call(bf16[512,1024]{1,0:T(8,128)(2,1)} %tok.1, f32[1,2048]{1,0:T(1,128)} %bitcast.1, bf16[3,2048,1024]{2,1,0:T(8,128)(2,1)} %w_qkv.1, bf16[1024,2048]{1,0:T(8,128)(2,1)} %w_out.1), custom_call_target="tpu_custom_call" | custom-call | tf_op jit(solution)/shard_map/sublayer/pallas_call | solution.py:390
  133.9 2.3 %copy.6 = bf16[512,1024]{1,0:T(8,128)(2,1)} copy(bf16[512,1024]{1,0:T(8,128)(2,1)} %sublayer.1) | data formatting | bytes 2097152

commit v2 on v1

v2 whole, which is shorter than its diff:
```python
import functools
import math

import jax
import jax.numpy as jnp
from jax import lax
from jax.experimental import pallas as pl
from jax.experimental.pallas import tpu as pltpu
from jax.sharding import PartitionSpec as P

HEAD_DIM = 128
MESH = pl.DeviceIdType.MESH


def remote(src, dst, send, recv, seq, tp):
    return pltpu.make_async_remote_copy(
        src_ref=src, dst_ref=dst, send_sem=send, recv_sem=recv, device_id=(seq, tp), device_id_type=MESH
    )


def put(src, dst, send, recv, seq, tp, own):
    @pl.when(own)
    def _():
        pltpu.make_async_copy(src, dst, recv).start()

    @pl.when(jnp.logical_not(own))
    def _():
        remote(src, dst, send, recv, seq, tp).start()


def barrier_wait(barrier, count):
    pl.semaphore_wait(barrier, count)


def half_kernel(
    n, heads, tok, gain_ref, w_qkv, w_out, out,
    pair, far, normed, first, wbuf, wout, xq, xk, xv, yq, yk, yv, q_all, k_all, v_all, acc, top, s0, s1, ctx, held, sent, came,
    kept, res, gain, lsem, swap, wsem, xsem, osem, qsend, qrecv, fsend, frecv, csend, crecv, psem,
):
    me, core = lax.axis_index("seq"), lax.axis_index("tp")
    other = 1 - core
    rows, feats = pair.shape[1], pair.shape[2]
    plane, near = n // 4, n // 2
    groups = plane // 2
    piece = rows // groups
    layer, spot = me // plane, lax.rem(me, plane)
    side, inner = me // near, lax.rem(me // plane, 2)
    central = inner != side
    mate = (2 - side) * plane + spot
    lane = lax.rem(me, 2)
    head = side * plane + spot
    bf, f32 = jnp.bfloat16, jnp.float32

    barrier = pltpu.get_barrier_semaphore()

    def greet(i, carry):
        there = lax.rem(2 * me + core + i, 2 * n)
        pl.semaphore_signal(barrier, inc=1, device_id=(there // 2, lax.rem(there, 2)), device_id_type=MESH)
        return carry

    lax.fori_loop(1, 2 * n, greet, 0)
    mine = pltpu.make_async_copy(tok, pair.at[core], lsem.at[0])
    mine.start()
    trade = remote(tok, pair.at[core], swap.at[0], swap.at[1], me, other)

    def cut(c):
        return pl.ds(c * piece, piece)

    kind = 1 - central.astype(jnp.int32)

    def across(c, half, src=None):
        src = normed.at[half, cut(c)] if src is None else src
        return remote(src, far.at[kind, half, cut(c)], xsem.at[0, kind, c, half], xsem.at[1, kind, c, half], mate, core)

    def inside(which, c, half):
        ref = far.at[which, half, cut(c)]
        return remote(ref, ref, xsem.at[2, which, c, half], xsem.at[3, which, c, half], me, other)

    def sends_x(when):
        return jnp.logical_and(core == inner, when)

    def wcopy(j):
        at = pl.ds(pl.multiple_of(side * plane * HEAD_DIM, HEAD_DIM), plane * HEAD_DIM)
        return pltpu.make_async_copy(w_qkv.at[j, :, at], wbuf.at[j], wsem.at[j])

    for j in range(3):
        wcopy(j).start()
    fetch_out = pltpu.make_async_copy(w_out, wout, lsem.at[1])
    fetch_out.start()
    gain[...] = gain_ref[...].astype(f32).reshape(1, 2 * feats)
    acc[...] = jnp.zeros_like(acc)
    top[...] = jnp.full_like(top, -1e30)
    v_all[:, HEAD_DIM:, :] = jnp.ones((v_all.shape[0], v_all.shape[1] - HEAD_DIM, v_all.shape[2]), bf)
    barrier_wait(barrier, 2 * n - 1)
    trade.start()

    @pl.when(sends_x(central))
    def _():
        across(0, core, tok.at[cut(0)]).start()

    mine.wait()
    trade.wait()

    @pl.when(sends_x(central))
    def _():
        across(0, other, pair.at[other, cut(0)]).start()

    step = 32

    def normalize(src, dst, count):
        def norm(i, carry):
            to = pl.ds(pl.multiple_of(i * step, step), step)
            a = src[0, to, :].astype(f32)
            b = src[1, to, :].astype(f32)
            average = (jnp.sum(a, axis=1, keepdims=True) + jnp.sum(b, axis=1, keepdims=True)) / (2 * feats)
            second = (jnp.sum(a * a, axis=1, keepdims=True) + jnp.sum(b * b, axis=1, keepdims=True)) / (2 * feats)
            scale = lax.rsqrt(second - average * average + 1e-06)
            dst[0, to, :] = ((a - average) * scale * gain[0:1, :feats]).astype(bf)
            dst[1, to, :] = ((b - average) * scale * gain[0:1, feats:]).astype(bf)
            return carry

        lax.fori_loop(0, count // step, norm, 0)

    factor = HEAD_DIM ** (-0.5) * math.log2(math.e)

    def spots(block, u, i):
        if block == 0:
            k_at = u * plane + i
            return q_all.at[i], k_all.at[k_at], v_all.at[k_at, pl.ds(0, HEAD_DIM)]
        k_at = 2 * plane + 2 * (block - 1) + u
        at = pl.ds(pl.multiple_of(i * piece, piece), piece)
        return q_all.at[plane + block - 1, at], k_all.at[k_at, at], v_all.at[k_at, pl.ds(0, HEAD_DIM), at]

    def staged(block, h):
        if block == 0:
            return xq.at[h], xk.at[h], xv.at[h]
        return yq.at[block - 1, h], yk.at[block - 1, h], yv.at[block - 1, h]

    def moves(block, h, j):
        chip = side * near + core * plane + h
        own = jnp.logical_and(chip == me, core == lane)
        i = lax.rem(me, near) // 2 if block == 0 else spot // 2
        src, dst = staged(block, h)[j], spots(block, lane, i)[j]
        return (src, dst, qsend.at[block, h, j], qrecv.at[block, i, j], chip, lane), own

    def deliver(block, h, j):
        args, own = moves(block, h, j)
        put(*args, own)

    def delivered(block, h, j):
        args, own = moves(block, h, j)

        @pl.when(jnp.logical_not(own))
        def _():
            remote(*args).wait_send()

    def project(block, src):
        for j in range(3):
            if block == 0:
                wcopy(j).wait()
            got = jnp.dot(src[0], wbuf[j, :feats], preferred_element_type=f32)
            got = got + jnp.dot(src[1], wbuf[j, feats:], preferred_element_type=f32)
            if j == 0:
                got = got * factor
            for h in range(plane):
                part = got[:, h * HEAD_DIM : (h + 1) * HEAD_DIM]
                staged(block, h)[j][...] = (part.T if j == 2 else part).astype(bf)
            for turn in range(plane):
                deliver(block, lax.rem(spot + turn, plane), j)

    def wave(w):
        which, c = w // groups, w % groups

        @pl.when(central)
        def _():
            lands = core == (side if which == 0 else 1 - side)

            @pl.when(lands)
            def _():
                for half in range(2):
                    ref = far.at[which, half, cut(c)]
                    remote(ref, ref, xsem.at[0, which, c, half], xsem.at[1, which, c, half], mate, core).wait_recv()
                    inside(which, c, half).start()

            @pl.when(jnp.logical_not(lands))
            def _():
                for half in range(2):
                    inside(which, c, half).wait_recv()

            if w == 0:
                normalize(far.at[0, :, cut(0)], first, piece)
                project(1, first)
            else:
                project(w + 1, far.at[which, :, cut(c)])

    def wait_block(block, i):
        for j, (src, dst) in enumerate(zip(staged(block, 0), spots(block, core, i))):
            remote(src, dst, qsend.at[block, 0, j], qrecv.at[block, i, j], me, other).wait_recv()

    def share(slot, u, way):
        at = u * plane + slot if way == 0 else 2 * plane + 2 * slot + u
        sem = slot if way == 0 else plane + slot
        k_ref, v_ref = k_all.at[at], v_all.at[at, pl.ds(0, HEAD_DIM)]
        return (
            remote(k_ref, k_ref, fsend.at[sem, 0], frecv.at[sem, 0], me, other),
            remote(v_ref, v_ref, fsend.at[sem, 1], frecv.at[sem, 1], me, other),
        )

    def pass_on(slot, way):
        for copy in share(slot, core, way):
            copy.start()

    def from_other(slot, way):
        for copy in share(slot, other, way):
            copy.wait_recv()

    def segment(rects):
        total = sum(nq * nk for _, nq, _, nk in rects)

        def find(t):
            spot_q = spot_k = None
            before = 0
            for q0, nq, k0, nk in rects:
                a = q0 + (t - before) // nk
                b = k0 + lax.rem(t - before, nk)
                if spot_q is None:
                    spot_q, spot_k = a, b
                else:
                    spot_q = jnp.where(t >= before, a, spot_q)
                    spot_k = jnp.where(t >= before, b, spot_k)
                before += nq * nk
            return spot_q, spot_k

        def score(t, s):
            a, b = find(t)
            s[...] = lax.dot_general(k_all[b], q_all[a], (((1,), (1,)), ((), ())), preferred_element_type=f32)

        def weigh(t, s):
            a, b = find(t)
            now = s[...]
            was = top[a]
            high = jnp.maximum(was, jnp.max(now, axis=0, keepdims=True))
            p = jnp.exp2((now - high).astype(bf))
            add = jnp.dot(v_all[b], p, preferred_element_type=f32)
            acc[a] = acc[a] * jnp.exp2(was - high) + add
            top[a] = high

        score(jnp.int32(0), s0)

        def body(i, carry):
            t = 2 * i
            score(t + 1, s1)
            weigh(t, s0)
            score(jnp.minimum(t + 2, total - 1), s0)
            weigh(t + 1, s1)
            return carry

        lax.fori_loop(0, total // 2, body, 0)
        if total % 2:
            weigh(jnp.int32(total - 1), s0)

    def place(l, at):
        return held.at[at, pl.ds(pl.multiple_of(l * HEAD_DIM, HEAD_DIM), HEAD_DIM)]

    def returns(b):
        if b < plane:
            s = side * near + 2 * b + core
            own = jnp.logical_and(s == me, inner == core)
            return [((ctx.at[b], place(head, pl.ds(0, rows)), csend.at[b, 0], crecv.at[head, 0], s, inner), own)]
        w = b - plane
        which, c = w // groups, w % groups
        home = (2 - side) if which == 0 else 3 * (1 - side)
        return [
            ((ctx.at[b, cut(i)], place(head, cut(c)), csend.at[b, i], crecv.at[head, c], home * plane + 2 * i + core, inner), None)
            for i in range(groups)
        ]

    def finish(start, count):
        def one(b, carry):
            t = acc[b]
            ctx[b] = (t[:HEAD_DIM] / t[HEAD_DIM : HEAD_DIM + 1]).T.astype(bf)
            return carry

        lax.fori_loop(start, start + count, one, 0)
        for b in range(start, start + count):
            for args, own in returns(b):
                if own is None:
                    remote(*args).start()
                else:
                    put(*args, own)

    normalize(pair, normed, rows)

    @pl.when(sends_x(central))
    def _():
        for c in range(1, groups):
            for half in range(2):
                across(c, half).start()

    project(0, normed)

    wave(0)
    here, there = groups * inner, groups * (1 - inner)
    for k in range(groups):
        wait_block(0, here + k)
        pass_on(here + k, 0)

    @pl.when(sends_x(jnp.logical_not(central)))
    def _():
        for c in range(groups):
            for half in range(2):
                across(c, half).start()

    segment([(here, groups, core * plane + here, groups)])
    wave(1)
    for k in range(groups):
        wait_block(0, there + k)
        pass_on(there + k, 0)
    segment([(here, groups, core * plane + there, groups), (there, groups, core * plane, plane)])
    for k in range(plane):
        from_other(k, 0)
    segment([(0, plane, other * plane, plane)])
    wave(2)

    def take(w):
        for i in range(groups):
            wait_block(w + 1, i)
        pass_on(w, 1)

    base = 2 * plane
    take(0)
    segment([(plane, 1, 0, base)])
    from_other(0, 1)
    segment([(plane, 1, base, 2), (0, plane, base, 2)])
    wave(3)
    take(1)
    segment([(plane + 1, 1, 0, base + 2), (plane, 2, base + 2 + core, 1)])
    from_other(1, 1)
    segment([(plane, 2, base + 2 + other, 1), (0, plane, base + 2, 2)])
    take(2)
    segment([(plane + 2, 1, 0, base + 4), (plane, 3, base + 4 + core, 1)])
    from_other(2, 1)
    take(3)
    segment([(plane, 3, base + 4 + other, 1), (plane, 3, base + 6 + core, 1)])
    from_other(3, 1)
    segment([(plane, 3, base + 6 + other, 1)])
    finish(plane, plane - 1)
    segment([(plane + 3, 1, 0, base + 8)])
    finish(plane + 3, 1)
    for half in range(2):
        segment([(half * groups, groups, base + 4, 4)])
        finish(half * groups, groups)

    fetch_out.wait()
    for k in range(plane):
        l = side * plane + k
        remote(ctx.at[0], place(l, pl.ds(0, rows)), csend.at[0, 0], crecv.at[l, 0], me, other).wait_recv()

    def product(half, c):
        at = pl.ds(pl.multiple_of(half * feats, feats), feats)
        return jnp.dot(held[c * piece : (c + 1) * piece, :], wout[:, at], preferred_element_type=f32)

    def hand(c):
        return remote(sent.at[c], came.at[c], psem.at[0, c], psem.at[1, c], me, other)

    def leave(c):
        return pltpu.make_async_copy(res.at[cut(c)], out.at[cut(c)], osem.at[c])

    for c in range(groups):
        for k in range(plane):
            l = (1 - side) * plane + k
            remote(ctx.at[0, cut(c)], place(l, cut(c)), csend.at[0, 0], crecv.at[l, c], me, other).wait_recv()
        sent[c] = product(other, c).astype(bf)
        hand(c).start()
        kept[c * piece : (c + 1) * piece, :] = product(core, c)

    for c in range(groups):
        hand(c).wait_recv()
        at = slice(c * piece, (c + 1) * piece)
        res[at, :] = (pair[core, at, :].astype(f32) + (kept[at, :] + came[c].astype(f32))).astype(bf)
        leave(c).start()

    for h in range(plane):
        for j in range(3):
            delivered(0, h, j)

    @pl.when(central)
    def _():
        for block in range(1, plane + 1):
            for h in range(plane):
                for j in range(3):
                    delivered(block, h, j)
        for which in range(2):
            lands = core == (side if which == 0 else 1 - side)

            @pl.when(lands)
            def _():
                for c in range(groups):
                    for half in range(2):
                        inside(which, c, half).wait_send()

    for slot in range(plane):
        for way in range(2):
            for copy in share(slot, core, way):
                copy.wait_send()

    @pl.when(core == inner)
    def _():
        for c in range(groups):
            for half in range(2):
                across(c, half).wait_send()

    for b in range(2 * plane):
        for args, own in returns(b):
            if own is None:
                remote(*args).wait_send()
            else:

                @pl.when(jnp.logical_not(own))
                def _():
                    remote(*args).wait_send()

    for c in range(groups):
        hand(c).wait_send()
        leave(c).wait()


def half_per_layer(n, tokens, ln_gain, w_qkv, w_out):
    rows, feats = tokens.shape
    heads = w_qkv.shape[2] // HEAD_DIM
    plane = n // 4
    groups = plane // 2
    piece = rows // groups
    bf, f32 = jnp.bfloat16, jnp.float32
    dma = pltpu.SemaphoreType.DMA
    chunks, blocks = 4 * plane, 2 * plane
    extra = HEAD_DIM + 16
    vmem = pltpu.VMEM
    hbm = pl.BlockSpec(memory_space=pltpu.HBM)
    return pl.pallas_call(
        functools.partial(half_kernel, n, heads),
        out_shape=jax.ShapeDtypeStruct((rows, feats), bf),
        in_specs=[hbm, pl.BlockSpec(memory_space=pltpu.VMEM), hbm, hbm],
        out_specs=hbm,
        scratch_shapes=[
            vmem((2, rows, feats), bf),
            vmem((2, 2, rows, feats), bf),
            vmem((2, rows, feats), bf),
            vmem((2, piece, feats), bf),
            vmem((3, 2 * feats, plane * HEAD_DIM), bf),
            vmem(w_out.shape, bf),
            vmem((plane, rows, HEAD_DIM), bf),
            vmem((plane, rows, HEAD_DIM), bf),
            vmem((plane, HEAD_DIM, rows), bf),
            vmem((plane, plane, piece, HEAD_DIM), bf),
            vmem((plane, plane, piece, HEAD_DIM), bf),
            vmem((plane, plane, HEAD_DIM, piece), bf),
            vmem((blocks, rows, HEAD_DIM), bf),
            vmem((chunks, rows, HEAD_DIM), bf),
            vmem((chunks, extra, rows), bf),
            vmem((blocks, extra, rows), f32),
            vmem((blocks, 1, rows), f32),
            vmem((rows, rows), f32),
            vmem((rows, rows), f32),
            vmem((blocks, rows, HEAD_DIM), bf),
            vmem((rows, heads * HEAD_DIM), bf),
            vmem((groups, piece, feats), bf),
            vmem((groups, piece, feats), bf),
            vmem((rows, feats), f32),
            vmem((rows, feats), bf),
            vmem((1, 2 * feats), f32),
            dma((2,)), dma((2,)), dma((3,)), dma((4, 2, groups, 2)), dma((groups,)),
            dma((plane + 1, plane, 3)), dma((plane + 1, plane, 3)), dma((blocks, 2)), dma((blocks, 2)),
            dma((blocks, groups)), dma((heads, groups)), dma((2, groups)),
        ],
        compiler_params=pltpu.CompilerParams(collective_id=0, has_side_effects=True, vmem_limit_bytes=60 * 1024 * 1024),
        name="sublayer",
    )(tokens, ln_gain, w_qkv, w_out)


def attend_block(totals, queries, block_kv, factor):
    running, denoms, accum = totals
    heads_here = queries.shape[1]
    keys_part = block_kv[0].reshape(block_kv.shape[1], heads_here, queries.shape[2])
    vals_part = block_kv[1].reshape(block_kv.shape[1], heads_here, queries.shape[2])
    scores = (
        jnp.einsum("thc,shc->ths", queries, keys_part, preferred_element_type=jnp.float32) * factor
    )
    highest = jnp.maximum(running, jnp.max(scores, axis=2))
    expon = jnp.exp(scores - highest[:, :, None])
    denoms = jnp.sum(expon, axis=2)
    weights = expon.astype(jnp.bfloat16)
    accum = jnp.einsum("ths,shc->thc", weights, vals_part, preferred_element_type=jnp.float32)
    return (highest, denoms, accum)


def start_totals(rows, heads_count):
    return (
        jnp.full((rows, heads_count), -1e30, jnp.float32),
        jnp.zeros((rows, heads_count), jnp.float32),
        jnp.zeros((rows, heads_count, HEAD_DIM), jnp.float32),
    )


def on_device(tokens, ln_gain, w_qkv, w_out):
    tok_rows = tokens.shape[0]
    whole = lax.all_gather(tokens, "tp", axis=1, tiled=True)
    values = whole.astype(jnp.float32)
    average = jnp.mean(values, axis=1, keepdims=True)
    second = jnp.mean(values * values, axis=1, keepdims=True)
    normed = (
        (values - average)
        * lax.rsqrt(second - average * average + 1e-06)
        * ln_gain.astype(jnp.float32)
    ).astype(jnp.bfloat16)
    projected = jnp.einsum("td,jdc->jtc", normed, w_qkv, preferred_element_type=jnp.float32).astype(
        jnp.bfloat16
    )
    heads_here = w_qkv.shape[2] // HEAD_DIM
    factor = HEAD_DIM ** (-0.5)
    queries = projected[0].reshape(tok_rows, heads_here, HEAD_DIM)
    keys_vals = projected[1:3]
    initial = start_totals(tok_rows, heads_here)
    final = attend_block(
        initial, queries, lax.all_gather(keys_vals, "seq", axis=1, tiled=True), factor
    )
    context = (
        (final[2] / final[1][:, :, None])
        .reshape(tok_rows, heads_here * HEAD_DIM)
        .astype(jnp.bfloat16)
    )
    summed = lax.psum_scatter(
        lax.dot_general(
            w_out, context, (((0,), (1,)), ((), ())), preferred_element_type=jnp.float32
        ).astype(jnp.bfloat16),
        "tp",
        scatter_dimension=0,
        tiled=True,
    ).astype(jnp.float32)
    return (tokens.astype(jnp.float32) + summed.T).astype(jnp.bfloat16)


def solution(mesh):
    in_specs = (P("seq", "tp"), P(), P(None, None, "tp"), P("tp", None))
    out_specs = P("seq", "tp")
    n, cores = mesh.shape["seq"], mesh.shape["tp"]

    def run(tokens, ln_gain, w_qkv, w_out):
        heads = w_qkv.shape[2] // HEAD_DIM
        if cores == 2 and heads * cores == n and n % 8 == 0 and tokens.shape[0] % n == 0:
            return half_per_layer(n, tokens, ln_gain, w_qkv, w_out)
        return on_device(tokens, ln_gain, w_qkv, w_out)

    return jax.shard_map(run, mesh=mesh, in_specs=in_specs, out_specs=out_specs, check_vma=False)
```

time: 138 us -> 117 us (0.85)
  Pallas kernels: 133 us -> 114 us
    pallas_call x1, Pallas kernels: 133 us -> 114 us  [half_per_layer(): pl.pallas_call(functools.partial(half_kernel, n, heads), out_shape=jax.Sh...]
where the time goes in v2:
time: 117 us; the launch traced here: 116 us
  Pallas kernels  114 us (97%)
  local copies, waits for them, and re-layouts  2.26 us (2%)
    pallas_call x1, Pallas kernels, half_per_layer(): pl.pallas_call(functools.partial(half_kernel, n, heads), out_shape=jax.Sh...  114 us

profile of v2, /device:TPU:29, one launch (start us, length us, event | category | flops | bytes accessed | tf_op | source)
XLA Modules:
  0.0 116.4 jit_solution(2143643750456327171)
XLA Ops:
  0.0 114.2 %sublayer.1 = bf16[512,1024]{1,0:T(8,128)(2,1)} custom-call(bf16[512,1024]{1,0:T(8,128)(2,1)} %tok.1, bf16[2048]{0:T(1024)(128)(2,1)} %gain_ref.1, bf16[3,2048,1024]{2,1,0:T(8,128)(2,1)} %w_qkv.1, bf16[1024,2048]{1,0:T(8,128)(2,1)} %w_out.1), custom_call_target="tpu_custom_call" | custom-call | tf_op jit(solution)/shard_map/sublayer/pallas_call | solution.py:440
  114.2 2.3 %copy.6 = bf16[512,1024]{1,0:T(8,128)(2,1)} copy(bf16[512,1024]{1,0:T(8,128)(2,1)} %sublayer.1) | data formatting | bytes 2097152

commit v3 on v2

--- a/solution.py
+++ b/solution.py
@@ -119,7 +119,7 @@
             dst[1, to, :] = ((b - average) * scale * gain[0:1, feats:]).astype(bf)
             return carry
 
-        lax.fori_loop(0, count // step, norm, 0)
+        lax.fori_loop(0, count // step, norm, 0, unroll=2)
 
     factor = HEAD_DIM ** (-0.5) * math.log2(math.e)
 
@@ -168,21 +168,25 @@
             for turn in range(plane):
                 deliver(block, lax.rem(spot + turn, plane), j)
 
+    def landing(which):
+        return core == (side if which == 0 else 1 - side)
+
+    def relay(w):
+        which, c = w // groups, w % groups
+
+        @pl.when(jnp.logical_and(central, landing(which)))
+        def _():
+            for half in range(2):
+                ref = far.at[which, half, cut(c)]
+                remote(ref, ref, xsem.at[0, which, c, half], xsem.at[1, which, c, half], mate, core).wait_recv()
+                inside(which, c, half).start()
+
     def wave(w):
         which, c = w // groups, w % groups
 
         @pl.when(central)
         def _():
-            lands = core == (side if which == 0 else 1 - side)
-
-            @pl.when(lands)
-            def _():
-                for half in range(2):
-                    ref = far.at[which, half, cut(c)]
-                    remote(ref, ref, xsem.at[0, which, c, half], xsem.at[1, which, c, half], mate, core).wait_recv()
-                    inside(which, c, half).start()
-
-            @pl.when(jnp.logical_not(lands))
+            @pl.when(jnp.logical_not(landing(which)))
             def _():
                 for half in range(2):
                     inside(which, c, half).wait_recv()
@@ -299,24 +303,28 @@
 
     project(0, normed)
 
+    relay(0)
     wave(0)
     here, there = groups * inner, groups * (1 - inner)
     for k in range(groups):
         wait_block(0, here + k)
         pass_on(here + k, 0)
 
+    segment([(here, groups, core * plane + here, groups)])
+    relay(1)
+    for k in range(groups):
+        wait_block(0, there + k)
+        pass_on(there + k, 0)
+
     @pl.when(sends_x(jnp.logical_not(central)))
     def _():
         for c in range(groups):
             for half in range(2):
                 across(c, half).start()
-
-    segment([(here, groups, core * plane + here, groups)])
+    segment([(here, groups, core * plane + there, groups)])
     wave(1)
-    for k in range(groups):
-        wait_block(0, there + k)
-        pass_on(there + k, 0)
-    segment([(here, groups, core * plane + there, groups), (there, groups, core * plane, plane)])
+    segment([(there, groups, core * plane, plane)])
+    relay(2)
     for k in range(plane):
         from_other(k, 0)
     segment([(0, plane, other * plane, plane)])
@@ -331,6 +339,7 @@
     take(0)
     segment([(plane, 1, 0, base)])
     from_other(0, 1)
+    relay(3)
     segment([(plane, 1, base, 2), (0, plane, base, 2)])
     wave(3)
     take(1)

time: 117 us -> 115 us (0.983)
  Pallas kernels: 114 us -> 112 us
    pallas_call x1, Pallas kernels: 114 us -> 112 us  [half_per_layer(): pl.pallas_call(functools.partial(half_kernel, n, heads), out_shape=jax.Sh...]
where the time goes in v3:
time: 115 us
  Pallas kernels  112 us (97%)
  local copies, waits for them, and re-layouts  2.26 us (2%)
    pallas_call x1, Pallas kernels, half_per_layer(): pl.pallas_call(functools.partial(half_kernel, n, heads), out_shape=jax.Sh...  112 us

profile of v3, /device:TPU:29, one launch (start us, length us, event | category | flops | bytes accessed | tf_op | source)
XLA Modules:
  0.0 114.6 jit_solution(1348711985290146107)
XLA Ops:
  0.0 112.3 %sublayer.1 = bf16[512,1024]{1,0:T(8,128)(2,1)} custom-call(bf16[512,1024]{1,0:T(8,128)(2,1)} %tok.1, bf16[2048]{0:T(1024)(128)(2,1)} %gain_ref.1, bf16[3,2048,1024]{2,1,0:T(8,128)(2,1)} %w_qkv.1, bf16[1024,2048]{1,0:T(8,128)(2,1)} %w_out.1), custom_call_target="tpu_custom_call" | custom-call | tf_op jit(solution)/shard_map/sublayer/pallas_call | solution.py:449
  112.4 2.3 %copy.6 = bf16[512,1024]{1,0:T(8,128)(2,1)} copy(bf16[512,1024]{1,0:T(8,128)(2,1)} %sublayer.1) | data formatting | bytes 2097152

commit v4 on v3

--- a/solution.py
+++ b/solution.py
@@ -35,7 +35,7 @@
 def half_kernel(
     n, heads, tok, gain_ref, w_qkv, w_out, out,
     pair, far, normed, first, wbuf, wout, xq, xk, xv, yq, yk, yv, q_all, k_all, v_all, acc, top, s0, s1, ctx, held, sent, came,
-    kept, res, gain, lsem, swap, wsem, xsem, osem, qsend, qrecv, fsend, frecv, csend, crecv, psem,
+    kept, gone, res, gain, lsem, swap, wsem, xsem, osem, qsend, qrecv, fsend, frecv, csend, crecv, psem,
 ):
     me, core = lax.axis_index("seq"), lax.axis_index("tp")
     other = 1 - core
@@ -361,13 +361,12 @@
         finish(half * groups, groups)
 
     fetch_out.wait()
-    for k in range(plane):
-        l = side * plane + k
-        remote(ctx.at[0], place(l, pl.ds(0, rows)), csend.at[0, 0], crecv.at[l, 0], me, other).wait_recv()
-
-    def product(half, c):
+    deep = plane * HEAD_DIM
+
+    def product(part, half, c):
+        k_at = pl.ds(pl.multiple_of(part * deep, deep), deep)
         at = pl.ds(pl.multiple_of(half * feats, feats), feats)
-        return jnp.dot(held[c * piece : (c + 1) * piece, :], wout[:, at], preferred_element_type=f32)
+        return jnp.dot(held[cut(c), k_at], wout[k_at, at], preferred_element_type=f32)
 
     def hand(c):
         return remote(sent.at[c], came.at[c], psem.at[0, c], psem.at[1, c], me, other)
@@ -379,14 +378,19 @@
         for k in range(plane):
             l = (1 - side) * plane + k
             remote(ctx.at[0, cut(c)], place(l, cut(c)), csend.at[0, 0], crecv.at[l, c], me, other).wait_recv()
-        sent[c] = product(other, c).astype(bf)
+        gone[cut(c), :] = product(1 - side, other, c)
+        kept[cut(c), :] = product(1 - side, core, c) + pair[core, cut(c), :].astype(f32)
+    for k in range(plane):
+        l = side * plane + k
+        remote(ctx.at[0], place(l, pl.ds(0, rows)), csend.at[0, 0], crecv.at[l, 0], me, other).wait_recv()
+    for c in range(groups):
+        sent[c] = (gone[cut(c), :] + product(side, other, c)).astype(bf)
         hand(c).start()
-        kept[c * piece : (c + 1) * piece, :] = product(core, c)
-
+    for c in range(groups):
+        kept[cut(c), :] = kept[cut(c), :] + product(side, core, c)
     for c in range(groups):
         hand(c).wait_recv()
-        at = slice(c * piece, (c + 1) * piece)
-        res[at, :] = (pair[core, at, :].astype(f32) + (kept[at, :] + came[c].astype(f32))).astype(bf)
+        res[cut(c), :] = (kept[cut(c), :] + came[c].astype(f32)).astype(bf)
         leave(c).start()
 
     for h in range(plane):
@@ -476,6 +480,7 @@
             vmem((groups, piece, feats), bf),
             vmem((groups, piece, feats), bf),
             vmem((rows, feats), f32),
+            vmem((rows, feats), f32),
             vmem((rows, feats), bf),
             vmem((1, 2 * feats), f32),
             dma((2,)), dma((2,)), dma((3,)), dma((4, 2, groups, 2)), dma((groups,)),

time: 115 us -> 114 us (level)
  no operation moved by 1% of the time
where the time goes in v4:
time: 114 us
  Pallas kernels  111 us (97%)
  local copies, waits for them, and re-layouts  2.26 us (2%)
    pallas_call x1, Pallas kernels, half_per_layer(): pl.pallas_call(functools.partial(half_kernel, n, heads), out_shape=jax.Sh...  111 us

profile of v4, /device:TPU:29, one launch (start us, length us, event | category | flops | bytes accessed | tf_op | source)
XLA Modules:
  0.0 113.5 jit_solution(307196620661223674)
XLA Ops:
  0.0 111.2 %sublayer.1 = bf16[512,1024]{1,0:T(8,128)(2,1)} custom-call(bf16[512,1024]{1,0:T(8,128)(2,1)} %tok.1, bf16[2048]{0:T(1024)(128)(2,1)} %gain_ref.1, bf16[3,2048,1024]{2,1,0:T(8,128)(2,1)} %w_qkv.1, bf16[1024,2048]{1,0:T(8,128)(2,1)} %w_out.1), custom_call_target="tpu_custom_call" | custom-call | tf_op jit(solution)/shard_map/sublayer/pallas_call | solution.py:453
  111.3 2.3 %copy.6 = bf16[512,1024]{1,0:T(8,128)(2,1)} copy(bf16[512,1024]{1,0:T(8,128)(2,1)} %sublayer.1) | data formatting | bytes 2097152
